TPU v7x, 32 devices: a whole 2x2x4 slice. The times are simulated.
32 devices in a mesh: groups: 2 (over x), dev: 16 (over z, y, core).
Axes of the slice: x: 2, y: 2, z: 4, core: 2. Of those that a mesh axis runs over, the one named last changes fastest.
Arguments:
- queries: bfloat16 [32, 512, 512], P(('groups', 'dev')), parts along dimension 0, may hold values from -120 to 120
- key_values: bfloat16 [2, 32, 512, 128], P(None, ('groups', 'dev')), parts along dimension 1, may hold values from -4 to 4
- lengths: int32 [4], P('groups'), parts along dimension 0, may hold values from 1 to 512, as said below
- out_proj: bfloat16 [4096, 2048], P('dev'), may hold values from -0.09375 to 0.09375
- residual: bfloat16 [32, 64, 2048], P(('groups', 'dev')), parts along dimension 0, may hold values from -8 to 8
- norm_gain: bfloat16 [2048], replicated, may hold values from 0.25 to 1.75
- router: bfloat16 [2048, 16], replicated, may hold values from -0.125 to 0.125
- expert_ids: int32 [32, 64, 8], P(('groups', 'dev')), parts along dimension 0, may hold values from 0 to 15, all different within a row; in each aligned block of 64 rows (0 to 63, 64 to 127, ..., all dimensions but the last counted through in order) at most 48 rows name the same one
- expert_gate_up: bfloat16 [16, 2048, 1536], P('dev'), may hold values from -0.125 to 0.125
- expert_down: bfloat16 [16, 768, 2048], P('dev'), may hold values from -0.21875 to 0.21875
Outputs:
- output: bfloat16 [32, 64, 2048], P(('groups', 'dev')), parts along dimension 0
There are 2 independent parts, one for each index of `groups`. A program takes and returns all parts, laid end to end along the dimension named above; an argument that names none is the same for every part. Nothing has to cross between parts.
Inputs may be any that keep to these rules, and one draw needn't show every extreme that they name: `lengths`: in every draw some request has all 512 cache slots filled. Each token names 8 different experts. The tokens of one block of expert_ids name any one expert at most 48 times, and in every draw some block names some expert exactly 48 times.
All inputs are finite; a program needn't handle non-finite values.
Results may differ from a plain program's by a relative error of at most 0.011.
Values may be sent and summed in bfloat16 or wider, within the bound.
A program may use at most 128 MiB of HBM per device.

v0:
```python
import functools
import math

import jax
import jax.numpy as jnp
from jax import lax
from jax.experimental import pallas as pl
from jax.experimental.pallas import tpu as pltpu
from jax.sharding import PartitionSpec as P

HEAD_DIM = 128
FF = 768
TOK_DEV = 64
GROUP = 8
EPSILON = 1e-06
MESH = pl.DeviceIdType.MESH


def bit_count(number):
    return number.bit_length() - 1


def flipped(index, bits):
    for bit in bits:
        index = index + (1 - 2 * ((index // (1 << bit)) % 2)) * (1 << bit)
    return index


def subset(bits, number):
    return [bit for place, bit in enumerate(bits) if number >> place & 1]


def greet(me, bits):
    barrier = pltpu.get_barrier_semaphore()
    for bit in bits:
        pl.semaphore_signal(
            barrier, inc=1, device_id={"dev": flipped(me, [bit])}, device_id_type=MESH
        )
    pl.semaphore_wait(barrier, len(bits))


def scatter_steps(me, unit, part_no, order, cols, x_ref, recv, stage, send_sem, recv_sem, block_of):
    k = len(order)
    total = (1 << k) - 1
    first = [total - ((1 << (k - s)) - 1) for s in range(k)]

    def arrived(step, number):
        return pltpu.make_async_remote_copy(
            src_ref=recv.at[first[step] + number, :, cols],
            dst_ref=recv.at[first[step] + number, :, cols],
            send_sem=send_sem.at[part_no, first[step] + number],
            recv_sem=recv_sem.at[part_no, first[step] + number],
            device_id={"dev": flipped(me, [unit + order[step]])},
            device_id_type=MESH,
        )

    copies = []

    def send(step, only=None):
        for number in reversed(range(1 << (k - 1 - step))) if only is None else [only]:
            slot = first[step] + number
            flips = [order[step]] + subset(order[step + 1 :], number)
            block = block_of(flips)
            if step == 0:
                source = x_ref.at[block, :, cols]
            else:
                value = x_ref[block, :, cols].astype(jnp.float32)
                for earlier in range(step):
                    place = (1 << (step - earlier - 1)) + (number << (step - earlier))
                    arrived(earlier, place).wait_recv()
                    value = value + recv[first[earlier] + place, :, cols].astype(jnp.float32)
                spot = slot - first[1]
                stage[spot, :, cols] = value.astype(stage.dtype)
                source = stage.at[spot, :, cols]
            copy = pltpu.make_async_remote_copy(
                src_ref=source,
                dst_ref=recv.at[slot, :, cols],
                send_sem=send_sem.at[part_no, slot],
                recv_sem=recv_sem.at[part_no, slot],
                device_id={"dev": flipped(me, [unit + order[step]])},
                device_id_type=MESH,
            )
            copy.start()
            copies.append(copy)

    def finish(o_ref):
        value = x_ref[block_of([]), :, cols].astype(jnp.float32)
        for earlier in range(k):
            arrived(earlier, 0).wait_recv()
            value = value + recv[first[earlier], :, cols].astype(jnp.float32)
        o_ref[:, cols] = value
        for copy in copies:
            copy.wait_send()

    return send, finish


def scatter_kernel(unit, parts, bits, x_ref, o_ref, recv, stage, send_sem, recv_sem):
    me = lax.axis_index("dev")
    greet(me, [unit + bit for bit in bits])
    rank = me // (1 << unit)
    runs = [
        scatter_steps(
            me, unit, number, order, cols, x_ref, recv, stage, send_sem, recv_sem,
            lambda flips: flipped(rank, flips),
        )
        for number, (order, cols) in enumerate(parts)
    ]
    for step in range(len(bits)):
        for send, _ in runs:
            send(step)
    for _, finish in runs:
        finish(o_ref)


def attend_block(block, length, q_ref, halves, rows):
    heads = q_ref.shape[1] // HEAD_DIM
    picked = pl.ds(pl.multiple_of(block * rows, rows), rows)
    query = jnp.concatenate(
        [q_ref[picked, head * HEAD_DIM : (head + 1) * HEAD_DIM] for head in range(heads)], axis=0
    )
    scale = 1.0 / math.sqrt(HEAD_DIM)
    contract = (((1,), (1,)), ((), ()))
    old = lax.dot_general(query, halves[0, 0], contract, preferred_element_type=jnp.float32) * scale
    new = lax.dot_general(query, halves[1, 0], contract, preferred_element_type=jnp.float32) * scale
    column = lax.broadcasted_iota(jnp.int32, (1, old.shape[1]), 1)
    old = jnp.where(column < length, old, -1e30)
    column = lax.broadcasted_iota(jnp.int32, (rows, new.shape[1]), 1)
    token = lax.broadcasted_iota(jnp.int32, (rows, new.shape[1]), 0) + block * rows
    bias = jnp.where(column <= token, 0.0, -1e30)
    new = new + jnp.concatenate([bias] * heads, axis=0)
    top = jnp.maximum(jnp.max(old, axis=1, keepdims=True), jnp.max(new, axis=1, keepdims=True))
    old = jnp.exp(old - top)
    new = jnp.exp(new - top)
    total = jnp.sum(old, axis=1, keepdims=True) + jnp.sum(new, axis=1, keepdims=True)
    mixed = jnp.dot(old.astype(jnp.bfloat16), halves[0, 1], preferred_element_type=jnp.float32)
    mixed += jnp.dot(new.astype(jnp.bfloat16), halves[1, 1], preferred_element_type=jnp.float32)
    mixed = (mixed / total).astype(jnp.bfloat16)
    return jnp.concatenate(
        [mixed[head * rows : (head + 1) * rows] for head in range(heads)], axis=1
    )


def attention_kernel(
    unit, parts, bits,
    lengths_ref, q_ref, kv_ref, proj_ref, o_ref,
    halves, proj, heads, x, recv, stage,
    send_sem, recv_sem, kv_sem, proj_send, proj_recv, own_sem,
):
    me = lax.axis_index("dev")
    low = list(range(unit))
    mates = [flipped(me, subset(low, number)) for number in range(1, 1 << unit)]
    ranks = [flipped(me, [unit + bit]) for bit in bits]
    barrier = pltpu.get_barrier_semaphore()
    for other in mates + ranks:
        pl.semaphore_signal(barrier, inc=1, device_id={"dev": other}, device_id_type=MESH)
    request = me % (1 << unit)
    rank = me // (1 << unit)
    parity = rank % 2
    depth = proj_ref.shape[0]
    own_rows = pl.ds(pl.multiple_of(request * depth, depth), depth)
    own_half = pltpu.make_async_copy(kv_ref, halves.at[parity], own_sem.at[0])
    own_proj = pltpu.make_async_copy(proj_ref, proj.at[own_rows], own_sem.at[1])
    own_half.start()
    own_proj.start()
    pl.semaphore_wait(barrier, len(mates) + len(ranks))
    kv_copy = pltpu.make_async_remote_copy(
        src_ref=kv_ref,
        dst_ref=halves.at[parity],
        send_sem=kv_sem.at[0],
        recv_sem=kv_sem.at[1],
        device_id={"dev": ranks[0]},
        device_id_type=MESH,
    )
    kv_copy.start()
    proj_copies = []
    for place, other in enumerate(mates):
        copy = pltpu.make_async_remote_copy(
            src_ref=proj_ref,
            dst_ref=proj.at[own_rows],
            send_sem=proj_send.at[place],
            recv_sem=proj_recv.at[place],
            device_id={"dev": other},
            device_id_type=MESH,
        )
        copy.start()
        proj_copies.append(copy)
    own_half.wait()
    kv_copy.wait()

    blocks, rows, width = x.shape
    far = 1 << (len(bits) - 1)
    masks = sorted(range(blocks), key=lambda m: (-bin(m).count("1"), -(m & far), m))
    place_of = {mask: place for place, mask in enumerate(masks)}
    length = lengths_ref[request]
    runs = [
        scatter_steps(
            me, unit, number, order, cols, x, recv, stage, send_sem, recv_sem,
            lambda flips: place_of[sum(1 << bit for bit in flips)],
        )
        for number, (order, cols) in enumerate(parts)
    ]
    half = blocks // 2
    strip = math.gcd(width, 512)
    for group in range(2):
        for spot in range(half):
            mask = masks[group * half + spot]
            block = flipped(rank, subset(bits, mask))
            heads[spot * rows : (spot + 1) * rows, :] = attend_block(
                block, length, q_ref, halves, rows
            )
        if group == 0:
            own_proj.wait()
            for copy in proj_copies:
                copy.wait()
        for start in range(0, width, strip):
            product = jnp.dot(
                heads[...], proj[:, start : start + strip], preferred_element_type=jnp.float32
            ).astype(x.dtype)
            for spot in range(half):
                x[group * half + spot, :, start : start + strip] = product[
                    spot * rows : (spot + 1) * rows
                ]
        for spot in range(half):
            mask = masks[group * half + spot]
            for (send, _), (order, _) in zip(runs, parts):
                if mask >> order[0] & 1:
                    number = sum((mask >> bit & 1) << at for at, bit in enumerate(order[1:]))
                    send(0, number)
    for step in range(1, len(bits)):
        for send, _ in runs:
            send(step)
    for _, finish in runs:
        finish(o_ref)


def attention(lengths, queries, key_values, out_proj, unit, orders, collective_id):
    width = out_proj.shape[1]
    tokens, columns = queries.shape
    bits = sorted(orders[0])
    blocks = 1 << len(bits)
    rows = tokens // blocks
    cut = width * 3 // 4 // 128 * 128
    parts = [(orders[0], pl.ds(0, cut)), (orders[1], pl.ds(cut, width - cut))]
    mates = max((1 << unit) - 1, 1)
    kind = queries.dtype
    whole = pl.BlockSpec(memory_space=pltpu.VMEM)
    return pl.pallas_call(
        functools.partial(attention_kernel, unit, parts, bits),
        out_shape=jax.ShapeDtypeStruct((rows, width), jnp.float32),
        in_specs=[pl.BlockSpec(memory_space=pltpu.SMEM), whole, whole, whole],
        out_specs=whole,
        scratch_shapes=[
            pltpu.VMEM((2,) + key_values.shape, kind),
            pltpu.VMEM((out_proj.shape[0] << unit, width), kind),
            pltpu.VMEM((tokens // 2, columns), kind),
            pltpu.VMEM((blocks, rows, width), kind),
            pltpu.VMEM((blocks - 1, rows, width), kind),
            pltpu.VMEM((max(blocks // 2 - 1, 1), rows, width), kind),
            pltpu.SemaphoreType.DMA((2, blocks - 1)),
            pltpu.SemaphoreType.DMA((2, blocks - 1)),
            pltpu.SemaphoreType.DMA((2,)),
            pltpu.SemaphoreType.DMA((mates,)),
            pltpu.SemaphoreType.DMA((mates,)),
            pltpu.SemaphoreType.DMA((2,)),
        ],
        compiler_params=pltpu.CompilerParams(collective_id=collective_id, has_side_effects=True),
    )(lengths, queries, key_values, out_proj)


def reduce_scatter(x, unit, orders, collective_id):
    blocks, rows, width = x.shape
    bits = sorted(orders[0])
    cut = width * 3 // 4 // 128 * 128
    parts = [(orders[0], pl.ds(0, cut)), (orders[1], pl.ds(cut, width - cut))]
    return pl.pallas_call(
        functools.partial(scatter_kernel, unit, parts, bits),
        out_shape=jax.ShapeDtypeStruct((rows, width), jnp.float32),
        in_specs=[pl.BlockSpec(memory_space=pltpu.VMEM)],
        out_specs=pl.BlockSpec(memory_space=pltpu.VMEM),
        scratch_shapes=[
            pltpu.VMEM((blocks - 1, rows, width), x.dtype),
            pltpu.VMEM((max(blocks // 2 - 1, 1), rows, width), x.dtype),
            pltpu.SemaphoreType.DMA((2, blocks - 1)),
            pltpu.SemaphoreType.DMA((2, blocks - 1)),
        ],
        compiler_params=pltpu.CompilerParams(collective_id=collective_id, has_side_effects=True),
    )(x)


def gather_kernel(parts, bits, x_ref, g_ref, ox_ref, og_ref, send_sem, recv_sem, own_sem):
    me = lax.axis_index("dev")
    greet(me, bits)
    k = len(bits)
    pairs = [(x_ref, ox_ref), (g_ref, og_ref)]
    local = []
    for number, (source, target) in enumerate(pairs):
        copy = pltpu.make_async_copy(source, target.at[me], own_sem.at[number])
        copy.start()
        local.append(copy)
    sent = []

    def forward(part_no, held, step):
        which, order, cols = parts[part_no]
        source, target = pairs[which]
        block = flipped(me, subset(order, held))
        slot = (1 << step) - 1 + held
        copy = pltpu.make_async_remote_copy(
            src_ref=source.at[:, cols] if held == 0 else target.at[block, :, cols],
            dst_ref=target.at[block, :, cols],
            send_sem=send_sem.at[part_no, slot],
            recv_sem=recv_sem.at[part_no, slot],
            device_id={"dev": flipped(me, [order[step]])},
            device_id_type=MESH,
        )
        copy.start()
        sent.append(copy)

    def arrive(part_no, held, step):
        which, order, cols = parts[part_no]
        target = pairs[which][1]
        block = flipped(me, subset(order, held) + [order[step]])
        slot = (1 << step) - 1 + held
        pltpu.make_async_remote_copy(
            src_ref=target.at[block, :, cols],
            dst_ref=target.at[block, :, cols],
            send_sem=send_sem.at[part_no, slot],
            recv_sem=recv_sem.at[part_no, slot],
            device_id={"dev": flipped(me, [order[step]])},
            device_id_type=MESH,
        ).wait_recv()

    for step in range(k):
        for part_no in range(len(parts)):
            forward(part_no, 0, step)
    for step in range(k):
        for held in range(1 << step):
            for part_no in range(len(parts)):
                arrive(part_no, held, step)
                for later in range(step + 1, k):
                    forward(part_no, held + (1 << step), later)
    for copy in local:
        copy.wait()
    for copy in sent:
        copy.wait_send()


def all_gather(x, gates, orders, collective_id):
    rows, width = x.shape
    bits = sorted(orders[0])
    count = 1 << len(bits)
    cut = width * 3 // 4 // 128 * 128
    parts = [
        (1, orders[0], pl.ds(0, gates.shape[1])),
        (0, orders[0], pl.ds(0, cut)),
        (0, orders[1], pl.ds(cut, width - cut)),
    ]
    return pl.pallas_call(
        functools.partial(gather_kernel, parts, bits),
        out_shape=[
            jax.ShapeDtypeStruct((count, rows, width), x.dtype),
            jax.ShapeDtypeStruct((count,) + gates.shape, gates.dtype),
        ],
        in_specs=[pl.BlockSpec(memory_space=pltpu.VMEM)] * 2,
        out_specs=[pl.BlockSpec(memory_space=pltpu.VMEM)] * 2,
        scratch_shapes=[
            pltpu.SemaphoreType.DMA((3, count - 1)),
            pltpu.SemaphoreType.DMA((3, count - 1)),
            pltpu.SemaphoreType.DMA((2,)),
        ],
        compiler_params=pltpu.CompilerParams(collective_id=collective_id, has_side_effects=True),
    )(x, gates)


def swapped(order, one, two):
    order = list(order)
    order[one], order[two] = order[two], order[one]
    return order


def per_device(
    queries,
    key_values,
    lengths,
    out_proj,
    residual,
    norm_gain,
    router,
    expert_ids,
    expert_gate_up,
    expert_down,
):
    devices = lax.axis_size("dev")
    my_index = lax.axis_index("dev")
    width = residual.shape[-1]
    requests_n = devices // GROUP
    low_bits = bit_count(requests_n)
    near = list(range(bit_count(GROUP)))
    attended = attention(
        lengths, queries[0], key_values[:, 0], out_proj, low_bits, [near, swapped(near, 0, 1)], 1
    )
    stream = (residual[0].astype(jnp.float32) + attended).astype(jnp.bfloat16)
    values = stream.astype(jnp.float32)
    normed = (
        values
        * lax.rsqrt(jnp.mean(values * values, axis=-1, keepdims=True) + EPSILON)
        * norm_gain.astype(jnp.float32)
    ).astype(jnp.bfloat16)
    logits = jnp.dot(normed, router, preferred_element_type=jnp.float32)
    experts_n = router.shape[1]
    token_ids = expert_ids[0]
    named = jnp.any(token_ids[..., None] == jnp.arange(experts_n, dtype=jnp.int32), axis=1)
    raised_gate = jnp.where(named, jnp.exp(logits), 0.0)
    gates = raised_gate / jnp.sum(raised_gate, axis=-1, keepdims=True)
    lanes = -(-TOK_DEV // 128) * 128
    gates = jnp.pad(gates.T, ((0, 0), (0, lanes - TOK_DEV)))
    every = list(range(bit_count(devices)))
    far = every[::-1]
    count = len(far)
    rows_all, gates_all = all_gather(normed, gates, [far, swapped(far, count - 3, count - 2)], 2)
    my_gates = lax.dynamic_index_in_dim(gates_all, my_index, 1, keepdims=False)[:, :TOK_DEV]
    flat_rows = rows_all.reshape(devices * TOK_DEV, width)
    projected = jnp.dot(flat_rows, expert_gate_up[0], preferred_element_type=jnp.float32)
    activation = (jax.nn.silu(projected[:, :FF]) * projected[:, FF:]).astype(jnp.bfloat16)
    produced = jnp.dot(activation, expert_down[0], preferred_element_type=jnp.float32)
    weighted = (my_gates.reshape(-1, 1) * produced).astype(jnp.bfloat16)
    weighted = weighted.reshape(devices, TOK_DEV, width)
    combined = reduce_scatter(weighted, 0, [every, swapped(every, 1, 2)], 3)
    return (values + combined).astype(jnp.bfloat16)[None]


def solution(mesh):
    return jax.shard_map(
        per_device,
        mesh=mesh,
        in_specs=(
            P(("groups", "dev"), None, None),
            P(None, ("groups", "dev"), None, None),
            P("groups"),
            P("dev", None),
            P(("groups", "dev"), None, None),
            P(),
            P(),
            P(("groups", "dev"), None, None),
            P("dev", None, None),
            P("dev", None, None),
        ),
        out_specs=P(("groups", "dev"), None, None),
        check_vma=False,
    )
```

profile of v0, /device:TPU:0, one launch (start us, length us, event | category | flops | bytes accessed | tf_op | source)
XLA Modules:
  0.0 133.6 jit_solution(811252687695542961)
XLA Ops:
  0.0 0.0 copy-start
  0.0 0.9 fusion.13
  0.9 0.8 convert_element_type.33
  1.7 43.1 %shard_map.100 = f32[64,2048]{1,0:T(8,128)} custom-call(s32[2]{0:T(128)} %lengths_ref.1, bf16[512,512]{1,0:T(8,128)(2,1)} %bitcast.25, bf16[2,512,128]{2,1,0:T(8,128)(2,1)} %bitcast.26, bf16[256,2048]{1,0:T(8,128)(2,1)} %proj_ref.1), custom_call_target="tpu_custom_call" | custom-call | tf_op jit(solution)/shard_map/pallas_call | solution.py:248
  44.8 1.3 fusion.7
  46.1 0.0 copy-start.2
  46.1 0.7 copy-done.2
  46.8 0.1 fusion.9.x_ref
  46.9 0.0 copy-start.1
  46.9 1.1 fusion.16
  48.1 0.6 pad.4.g_ref
  48.7 0.0 copy-done.1
  48.7 32.7 %shard_map.101 = (bf16[16,64,2048]{2,1,0:T(8,128)(2,1)}, f32[16,16,128]{2,1,0:T(8,128)}) custom-call(bf16[64,2048]{1,0:T(8,128)(2,1)} %copy-done.1, f32[16,128]{1,0:T(8,128)} %pad.4.g_ref), custom_call_target="tpu_custom_call" | custom-call | tf_op jit(solution)/shard_map/pallas_call | solution.py:358
  81.4 0.9 constant_dynamic-slice_fusion
  82.2 0.1 mul.41
  82.3 10.0 %fusion = f32[1024,1536]{1,0:T(8,128)S(1)} fusion(bf16[1024,2048]{1,0:T(8,128)(2,1)} %bitcast.29, bf16[1,2048,1536]{2,1,0:T(8,128)(2,1)} %param.18), kind=kOutput, calls=%fused_computation.1 | convolution fusion | flops 6442450944 | bytes 16777216 | tf_op jit(solution)/shard_map/dot_general | solution.py:423
  92.3 0.0 copy-done
  92.3 5.0 %multiply_convert_fusion = bf16[1024,2048]{1,0:T(8,128)(2,1)} fusion(f32[1024]{0:T(1024)S(1)} %mul.41, bf16[1,768,2048]{2,1,0:T(8,128)(2,1)S(1)} %copy-done, f32[1024,1536]{1,0:T(8,128)S(1)} %fusion), kind=kOutput, calls=%fused_computation | convolution fusion | flops 3230138368 | bytes 13635584 | tf_op jit(solution)/shard_map/dot_general | solution.py:425
  97.4 0.0 copy-start.3
  97.4 34.4 %shard_map.102 = f32[64,2048]{1,0:T(8,128)} custom-call(bf16[16,64,2048]{2,1,0:T(8,128)(2,1)} %bitcast.24), custom_call_target="tpu_custom_call" | custom-call | tf_op jit(solution)/shard_map/pallas_call | solution.py:276
  131.8 0.0 copy-done.3
  131.8 1.8 %fusion.12 = bf16[1,64,2048]{2,1,0:T(8,128)(2,1)} fusion(f32[64,2048]{1,0:T(8,128)} %shard_map.102, bf16[64,2048]{1,0:T(8,128)(2,1)S(1)} %copy-done.3), kind=kLoop, calls=%fused_computation.18 | loop fusion | flops 393216 | bytes 1048576 | tf_op jit(solution)/shard_map/broadcast_in_dim | solution.py:429
  (2 shorter events, 0.0 us)
Async XLA Ops:
  0.0 92.3 %copy-start = (bf16[1,768,2048]{2,1,0:T(8,128)(2,1)S(1)}, bf16[1,768,2048]{2,1,0:T(8,128)(2,1)}, u32[]{:S(2)}) copy-start(bf16[1,768,2048]{2,1,0:T(8,128)(2,1)} %param.19) | copy-start | bytes 9437188
  46.1 0.7 copy-start.2
  46.9 1.8 %copy-start.1 = (bf16[64,2048]{1,0:T(8,128)(2,1)}, bf16[64,2048]{1,0:T(8,128)(2,1)S(1)}, u32[]{:S(2)}) copy-start(bf16[64,2048]{1,0:T(8,128)(2,1)S(1)} %fusion.9.x_ref) | copy-start | bytes 786436
  97.4 34.5 %copy-start.3 = (bf16[64,2048]{1,0:T(8,128)(2,1)S(1)}, bf16[64,2048]{1,0:T(8,128)(2,1)}, u32[]{:S(2)}) copy-start(bf16[64,2048]{1,0:T(8,128)(2,1)} %copy-done.2) | copy-start | bytes 786436
where the time goes:
time: 134 us
  Pallas kernels  110 us (82%)
  matrix products  16.2 us (12%)
  other arithmetic  4.87 us (4%)
  local copies, waits for them, and re-layouts  2.25 us (2%)
    pallas_call x1, Pallas kernels, attention(): pl.pallas_call(functools.partial(attention_kernel, unit, parts, bits), ou...  43.1 us
    pallas_call x1, Pallas kernels, reduce_scatter(): pl.pallas_call(functools.partial(scatter_kernel, unit, parts, bits), out_...  34.4 us
    pallas_call x1, Pallas kernels, all_gather(): pl.pallas_call(functools.partial(gather_kernel, parts, bits), out_shape=[...  32.7 us
    dot_general x1, matrix products, per_device(): jnp.dot(flat_rows, expert_gate_up[0], preferred_element_type=jnp.float32)  10 us
    dot_general x1, matrix products, per_device(): jnp.dot(activation, expert_down[0], preferred_element_type=jnp.float32)  5.05 us

commit v1 on v0

--- a/solution.py
+++ b/solution.py
@@ -14,6 +14,17 @@
 GROUP = 8
 EPSILON = 1e-06
 MESH = pl.DeviceIdType.MESH
+CHUNKS = 4
+AG_KINDS = (0, 1, 0, 0)
+RS_KINDS = (0, 1, 0, 0)
+AG_FIRST = 1.0
+AG_CHUNK = 1.0
+AG_HOP = 1.0
+FFN_START = 4.0
+FFN_CHUNK = 1.0
+FFN_SPAN = 0.9
+RS_LAG = 0.5
+RS_HOP = 1.0
 
 
 def bit_count(number):
@@ -372,6 +383,434 @@
     )(x, gates)
 
 
+def ag_time(k, stage):
+    return AG_CHUNK * k + AG_HOP * stage if stage else AG_FIRST * k
+
+
+def ffn_time(k, part):
+    return FFN_START + FFN_CHUNK * k + FFN_SPAN * part + 0.001
+
+
+def rs_time(k, stage):
+    return FFN_START + FFN_CHUNK * k + FFN_SPAN + RS_LAG + RS_HOP * stage
+
+
+def moe_fits(devices, rows, width, hidden):
+    if devices < 8 or rows % (16 * CHUNKS):
+        return False
+    weights = 3 * width * hidden
+    tokens = devices * rows * width
+    return 2 * (weights + 4 * tokens) < 48 * 2**20
+
+
+def moe_kernel(
+    line, ag_kinds, rs_kinds,
+    att_ref, res_ref, gain_ref, router_ref, ids_ref, gu_hbm, dn_hbm, o_ref,
+    gath, gu, dn, act, made, mrecv, part, yrecv, half, zrecv, held, ready,
+    w_sem, ag_send, ag_recv, m_send, m_recv, y_send, y_recv, z_send, z_recv,
+):
+    me = lax.axis_index("dev")
+    z, y, c = me // 4, (me // 2) % 2, me % 2
+    chunks, total, padded = gath.shape
+    rows, width = o_ref.shape
+    R = rows // chunks
+    hidden = dn.shape[0]
+    experts = router_ref.shape[0]
+    dest = [me + 4, me - 4, me + 2 - 4 * y, me + 1 - 2 * c]
+    allowed = [z + 1 < line, z > 0, None, None]
+    RIGHT, LEFT, YMATE, MATE = range(4)
+
+    def guarded(cond, body):
+        if cond is None:
+            body()
+        else:
+            pl.when(cond)(body)
+
+    def both(*conds):
+        conds = [cond for cond in conds if cond is not None]
+        if not conds:
+            return None
+        return functools.reduce(jnp.logical_and, conds)
+
+    copies = [
+        pltpu.make_async_copy(gu_hbm.at[0], gu, w_sem.at[0]),
+        pltpu.make_async_copy(dn_hbm.at[0], dn, w_sem.at[1]),
+    ]
+    for copy in copies:
+        copy.start()
+    barrier = pltpu.get_barrier_semaphore()
+    for way in range(4):
+        guarded(
+            allowed[way],
+            lambda way=way: pl.semaphore_signal(
+                barrier, inc=1, device_id={"dev": dest[way]}, device_id_type=MESH
+            ),
+        )
+
+    stream = (res_ref[...].astype(jnp.float32) + att_ref[...]).astype(jnp.bfloat16)
+    values = stream.astype(jnp.float32)
+    held[...] = values
+    scale = lax.rsqrt(jnp.mean(values * values, axis=-1, keepdims=True) + EPSILON)
+    normed = (values * scale * gain_ref[...].astype(jnp.float32).reshape(1, width)).astype(jnp.bfloat16)
+    logits = lax.dot_general(
+        router_ref[...], normed, (((1,), (1,)), ((), ())), preferred_element_type=jnp.float32
+    )
+    number = lax.broadcasted_iota(jnp.int32, (experts, rows), 0)
+    named = ids_ref[0:1, :] == number
+    for place in range(1, ids_ref.shape[0]):
+        named = jnp.logical_or(named, ids_ref[place : place + 1, :] == number)
+    raised = jnp.where(named, jnp.exp(logits), 0.0)
+    gates = raised / jnp.sum(raised, axis=0, keepdims=True)
+    high = gates.astype(jnp.bfloat16).astype(jnp.float32)
+    low = gates - high
+    spare = jnp.zeros((padded - width - 2 * experts, rows), jnp.float32)
+    extra = jnp.concatenate([high, low, spare], axis=0).T.astype(jnp.bfloat16)
+
+    def spot(core, column, place):
+        return pl.multiple_of(((core * 2 + column) * line + place) * R, R)
+
+    mine = pl.ds(spot(c, y, z), R)
+    for k in range(chunks):
+        gath[k, mine, 0:width] = normed[k * R : (k + 1) * R]
+        gath[k, mine, width:padded] = extra[k * R : (k + 1) * R]
+
+    pl.semaphore_wait(
+        barrier, 2 + (z > 0).astype(jnp.int32) + (z + 1 < line).astype(jnp.int32)
+    )
+
+    span = 2 * line - 1
+    started = []
+
+    def label(side, offset):
+        return side * span + offset + line - 1
+
+    def exists(offset):
+        if offset == 0:
+            return None
+        return z + offset >= 0 if offset < 0 else z + offset < line
+
+    def slab(k, side, offset):
+        column = y if side == 0 else 1 - y
+        return gath.at[k, pl.ds(spot(c, column, z + offset), R), :]
+
+    def ag_copy(k, side, offset, way):
+        if way == RIGHT:
+            landing = label(side, offset - 1)
+        elif way == LEFT:
+            landing = label(side, offset + 1)
+        elif way == YMATE:
+            landing = label(1 - side, offset)
+        else:
+            landing = 2 * span + label(side, offset)
+        where = slab(k, side, offset)
+        return pltpu.make_async_remote_copy(
+            src_ref=where, dst_ref=where,
+            send_sem=ag_send.at[k, label(side, offset), way],
+            recv_sem=ag_recv.at[k, landing],
+            device_id={"dev": dest[way]}, device_id_type=MESH,
+        )
+
+    def ag_ways(k, side, offset):
+        kind = ag_kinds[k]
+        ways = []
+        if kind == 0:
+            if side == 0:
+                if offset <= 0 and offset > 1 - line:
+                    ways.append(RIGHT)
+                if offset >= 0 and offset < line - 1:
+                    ways.append(LEFT)
+                ways.append(YMATE)
+        else:
+            if side == 0 and offset == 0:
+                ways.append(YMATE)
+            if offset <= 0 and offset > 1 - line:
+                ways.append(RIGHT)
+            if offset >= 0 and offset < line - 1:
+                ways.append(LEFT)
+        ways.append(MATE)
+        return ways
+
+    def ag_step(k, side, offset):
+        def body():
+            if side or offset:
+                arrived = slab(k, side, offset)
+                pltpu.make_async_remote_copy(
+                    src_ref=arrived, dst_ref=arrived,
+                    send_sem=ag_send.at[k, label(side, offset), MATE],
+                    recv_sem=ag_recv.at[k, label(side, offset)],
+                    device_id={"dev": dest[MATE]}, device_id_type=MESH,
+                ).wait_recv()
+            for way in ag_ways(k, side, offset):
+                copy = ag_copy(k, side, offset, way)
+                guarded(allowed[way], copy.start)
+
+        guarded(exists(offset), body)
+        for way in ag_ways(k, side, offset):
+            started.append(
+                (
+                    lambda way=way: both(exists(offset), allowed[way]),
+                    lambda way=way: ag_copy(k, side, offset, way),
+                )
+            )
+
+    def ag_stage(k, stage):
+        if stage == 0:
+            ag_step(k, 0, 0)
+            return
+        if stage < line:
+            ag_step(k, 0, -stage)
+            ag_step(k, 0, stage)
+        if stage == 1:
+            ag_step(k, 1, 0)
+        else:
+            ag_step(k, 1, 1 - stage)
+            ag_step(k, 1, stage - 1)
+
+    def mate_wait(k):
+        for side in range(2):
+            for offset in range(1 - line, line):
+                column = y if side == 0 else 1 - y
+
+                def body(side=side, offset=offset, column=column):
+                    where = gath.at[k, pl.ds(spot(1 - c, column, z + offset), R), :]
+                    pltpu.make_async_remote_copy(
+                        src_ref=where, dst_ref=where,
+                        send_sem=ag_send.at[k, label(side, offset), MATE],
+                        recv_sem=ag_recv.at[k, 2 * span + label(side, offset)],
+                        device_id={"dev": dest[MATE]}, device_id_type=MESH,
+                    ).wait_recv()
+
+                guarded(exists(offset), body)
+
+    core_rows = total // 2
+    strip = math.gcd(hidden, 256)
+
+    wide = math.gcd(width, 512)
+
+    def rise(k, start):
+        if start == 0:
+            if k == 0:
+                for copy in copies:
+                    copy.wait()
+            mate_wait(k)
+        x = gath[k, :, 0:width]
+        if True:
+            gate = jnp.dot(x, gu[:, start : start + strip], preferred_element_type=jnp.float32)
+            up = jnp.dot(
+                x, gu[:, hidden + start : hidden + start + strip],
+                preferred_element_type=jnp.float32,
+            )
+            act[:, start : start + strip] = (gate / (1.0 + jnp.exp(-gate)) * up).astype(act.dtype)
+
+    def fall(k, start):
+        tail = gath[k, :, width:padded].astype(jnp.float32)
+        lanes = lax.broadcasted_iota(jnp.int32, tail.shape, 1)
+        chosen = jnp.logical_or(lanes == me, lanes == me + experts)
+        weight = jnp.sum(jnp.where(chosen, tail, 0.0), axis=1, keepdims=True)
+        if True:
+            produced = jnp.dot(
+                act[...], dn[:, start : start + wide], preferred_element_type=jnp.float32
+            )
+            made[k, :, start : start + wide] = (weight * produced).astype(made.dtype)
+        if start + wide == width:
+            mate_copy(k).start()
+            started.append((lambda: None, lambda: mate_copy(k)))
+
+    def mate_copy(k):
+        theirs = pl.ds(pl.multiple_of((1 - c) * core_rows, core_rows), core_rows)
+        return pltpu.make_async_remote_copy(
+            src_ref=made.at[k, theirs, :], dst_ref=mrecv.at[k],
+            send_sem=m_send.at[k], recv_sem=m_recv.at[k],
+            device_id={"dev": dest[MATE]}, device_id_type=MESH,
+        )
+
+    def y_copy(k):
+        if rs_kinds[k] == 0:
+            source, target = part.at[k, 1 - y], yrecv.at[k]
+        else:
+            source, target = ready.at[k], yrecv.at[k, 0]
+        return pltpu.make_async_remote_copy(
+            src_ref=source, dst_ref=target,
+            send_sem=y_send.at[k], recv_sem=y_recv.at[k],
+            device_id={"dev": dest[YMATE]}, device_id_type=MESH,
+        )
+
+    def z_copy(k, target, way):
+        if rs_kinds[k] == 0:
+            source, landing = half.at[k, target], zrecv.at[k, way, target, 0]
+        else:
+            source, landing = part.at[k, :, target], zrecv.at[k, way, target]
+        return pltpu.make_async_remote_copy(
+            src_ref=source, dst_ref=landing,
+            send_sem=z_send.at[k, way, target], recv_sem=z_recv.at[k, way, target],
+            device_id={"dev": dest[way]}, device_id_type=MESH,
+        )
+
+    def merge(k):
+        mate_copy(k).wait_recv()
+        for column in range(2):
+            for place in range(line):
+                at = column * line + place
+                ours = pl.ds(pl.multiple_of(c * core_rows + at * R, R), R)
+                part[k, column, place] = (
+                    made[k, ours, :].astype(jnp.float32)
+                    + mrecv[k, at * R : (at + 1) * R, :].astype(jnp.float32)
+                ).astype(part.dtype)
+        if rs_kinds[k] == 0:
+            y_copy(k).start()
+            started.append((lambda: None, lambda: y_copy(k)))
+
+    def y_merge(k):
+        y_copy(k).wait_recv()
+        for place in range(line):
+            half[k, place] = (
+                part[k, y, place].astype(jnp.float32) + yrecv[k, place].astype(jnp.float32)
+            ).astype(half.dtype)
+
+    def z_hop(k, hop):
+        for way in (RIGHT, LEFT):
+            here = hop if way == RIGHT else line - 1 - hop
+            if way == RIGHT:
+                targets = range(line - 1, here, -1)
+            else:
+                targets = range(0, here)
+
+            def body(way=way, here=here, targets=targets):
+                for target in targets:
+                    if hop:
+                        z_copy(k, target, way).wait_recv()
+                        if rs_kinds[k] == 0:
+                            half[k, target] = (
+                                half[k, target].astype(jnp.float32)
+                                + zrecv[k, way, target, 0].astype(jnp.float32)
+                            ).astype(half.dtype)
+                        else:
+                            for column in range(2):
+                                part[k, column, target] = (
+                                    part[k, column, target].astype(jnp.float32)
+                                    + zrecv[k, way, target, column].astype(jnp.float32)
+                                ).astype(part.dtype)
+                    z_copy(k, target, way).start()
+
+            for target in targets:
+                started.append(
+                    (
+                        lambda here=here: z == here,
+                        lambda target=target, way=way: z_copy(k, target, way),
+                    )
+                )
+            pl.when(z == here)(body)
+
+    def gather_z(k, column):
+        where = pl.ds(k * R, R)
+
+        def take(way):
+            side = 0 if rs_kinds[k] == 0 else column
+            held[where, :] = held[where, :] + zrecv[k, way, z, side].astype(jnp.float32)
+
+        pl.when(z > 0)(lambda: take(RIGHT))
+        pl.when(z + 1 < line)(lambda: take(LEFT))
+
+    def wait_z(k):
+        pl.when(z > 0)(lambda: z_copy(k, z, RIGHT).wait_recv())
+        pl.when(z + 1 < line)(lambda: z_copy(k, z, LEFT).wait_recv())
+
+    def cross(k):
+        wait_z(k)
+        other = part[k, 1 - y, z].astype(jnp.float32)
+        from_left = zrecv[k, RIGHT, z, 1 - y].astype(jnp.float32)
+        from_right = zrecv[k, LEFT, z, 1 - y].astype(jnp.float32)
+        other = other + jnp.where(z > 0, from_left, 0.0)
+        other = other + jnp.where(z + 1 < line, from_right, 0.0)
+        ready[k] = other.astype(ready.dtype)
+        y_copy(k).start()
+        started.append((lambda: None, lambda: y_copy(k)))
+
+    def finish(k):
+        where = pl.ds(k * R, R)
+        if rs_kinds[k] == 0:
+            wait_z(k)
+            held[where, :] = held[where, :] + half[k, z].astype(jnp.float32)
+            gather_z(k, 0)
+            o_ref[where, :] = held[where, :].astype(o_ref.dtype)
+        else:
+            held[where, :] = held[where, :] + part[k, y, z].astype(jnp.float32)
+            gather_z(k, y)
+            y_copy(k).wait_recv()
+            o_ref[where, :] = (
+                held[where, :] + yrecv[k, 0].astype(jnp.float32)
+            ).astype(o_ref.dtype)
+
+    def rs_stages(k):
+        hops = [functools.partial(z_hop, k, hop) for hop in range(line - 1)]
+        if rs_kinds[k] == 0:
+            middle = [lambda: y_merge(k)] + hops
+        else:
+            middle = hops + [lambda: cross(k)]
+        return [lambda: merge(k)] + middle + [lambda: finish(k)]
+
+    pieces = [functools.partial(rise, start=start) for start in range(0, hidden, strip)]
+    pieces += [functools.partial(fall, start=start) for start in range(0, width, wide)]
+    agenda = []
+    for k in range(chunks):
+        for stage in range(line + 1):
+            agenda.append((ag_time(k, stage), lambda k=k, stage=stage: ag_stage(k, stage)))
+        for number, piece in enumerate(pieces):
+            agenda.append((ffn_time(k, number / len(pieces)), lambda k=k, piece=piece: piece(k)))
+        for number, step in enumerate(rs_stages(k)):
+            agenda.append((rs_time(k, number), step))
+    for _, step in sorted(agenda, key=lambda entry: entry[0]):
+        step()
+    for cond, copy in started:
+        guarded(cond(), lambda copy=copy: copy().wait_send())
+
+
+def moe(attended, residual, gain, router, ids, gate_up, down, collective_id):
+    devices = lax.axis_size("dev")
+    rows, width = residual.shape
+    hidden = down.shape[1]
+    experts = router.shape[0]
+    line = devices // 4
+    padded = width + -(-2 * experts // 128) * 128
+    R = rows // CHUNKS
+    kind = residual.dtype
+    span = 2 * line - 1
+    vmem = pl.BlockSpec(memory_space=pltpu.VMEM)
+    hbm = pl.BlockSpec(memory_space=pl.ANY)
+    dma = pltpu.SemaphoreType.DMA
+    total = devices * R
+    return pl.pallas_call(
+        functools.partial(moe_kernel, line, AG_KINDS, RS_KINDS),
+        out_shape=jax.ShapeDtypeStruct((rows, width), kind),
+        in_specs=[vmem] * 5 + [hbm] * 2,
+        out_specs=vmem,
+        scratch_shapes=[
+            pltpu.VMEM((CHUNKS, total, padded), kind),
+            pltpu.VMEM(gate_up.shape[1:], kind),
+            pltpu.VMEM(down.shape[1:], kind),
+            pltpu.VMEM((total, hidden), kind),
+            pltpu.VMEM((CHUNKS, total, width), kind),
+            pltpu.VMEM((CHUNKS, total // 2, width), kind),
+            pltpu.VMEM((CHUNKS, 2, line, R, width), kind),
+            pltpu.VMEM((CHUNKS, line, R, width), kind),
+            pltpu.VMEM((CHUNKS, line, R, width), kind),
+            pltpu.VMEM((CHUNKS, 2, line, 2, R, width), kind),
+            pltpu.VMEM((rows, width), jnp.float32),
+            pltpu.VMEM((CHUNKS, R, width), kind),
+            dma((2,)),
+            dma((CHUNKS, 2 * span, 4)),
+            dma((CHUNKS, 4 * span)),
+            dma((CHUNKS,)),
+            dma((CHUNKS,)),
+            dma((CHUNKS,)),
+            dma((CHUNKS,)),
+            dma((CHUNKS, 2, line)),
+            dma((CHUNKS, 2, line)),
+        ],
+        compiler_params=pltpu.CompilerParams(collective_id=collective_id, has_side_effects=True),
+    )(attended, residual, gain, router, ids, gate_up, down)
+
+
 def swapped(order, one, two):
     order = list(order)
     order[one], order[two] = order[two], order[one]
@@ -399,6 +838,11 @@
     attended = attention(
         lengths, queries[0], key_values[:, 0], out_proj, low_bits, [near, swapped(near, 0, 1)], 1
     )
+    if moe_fits(devices, TOK_DEV, width, FF):
+        return moe(
+            attended, residual[0], norm_gain, router.T, expert_ids[0].T,
+            expert_gate_up, expert_down, 2,
+        )[None]
     stream = (residual[0].astype(jnp.float32) + attended).astype(jnp.bfloat16)
     values = stream.astype(jnp.float32)
     normed = (

time: 134 us -> 122 us (0.910)
  matrix products: 16.2 us -> 0 us
  Pallas kernels: 110 us -> 120 us
  other arithmetic: 4.87 us -> 0 us
    dot_general x3 -> x0, matrix products: 16.2 us -> none  [the longest x1 10 us: per_device(): jnp.dot(flat_rows, expert_gate_up[0], preferred_element_type=jnp.float32)]
    pallas_call x2 -> x1, Pallas kernels: 67.1 us -> 76.9 us  [moe(): pl.pallas_call(functools.partial(moe_kernel, line, AG_KINDS, RS_KINDS), o...]
    broadcast_in_dim x1 -> x0, other arithmetic: 1.79 us -> none  [per_device(): return (values + combined).astype(jnp.bfloat16)[None]]
where the time goes in v1:
time: 122 us
  Pallas kernels  120 us (98%)
  local copies, waits for them, and re-layouts  1.67 us (1%)
    pallas_call x1, Pallas kernels, moe(): pl.pallas_call(functools.partial(moe_kernel, line, AG_KINDS, RS_KINDS), o...  76.9 us
    pallas_call x1, Pallas kernels, attention(): pl.pallas_call(functools.partial(attention_kernel, unit, parts, bits), ou...  43.1 us

profile of v1, /device:TPU:0, one launch (start us, length us, event | category | flops | bytes accessed | tf_op | source)
XLA Modules:
  0.0 121.7 jit_solution(3175896622984226961)
XLA Ops:
  0.0 43.1 %shard_map.100.att_ref = f32[64,2048]{1,0:T(8,128)} custom-call(s32[2]{0:T(128)} %lengths_ref.1, bf16[512,512]{1,0:T(8,128)(2,1)} %bitcast.9, bf16[2,512,128]{2,1,0:T(8,128)(2,1)} %bitcast.10, bf16[256,2048]{1,0:T(8,128)(2,1)} %proj_ref.1), custom_call_target="tpu_custom_call" | custom-call | tf_op jit(solution)/shard_map/pallas_call | solution.py:259
  43.1 76.9 %shard_map.101 = bf16[64,2048]{1,0:T(8,128)(2,1)} custom-call(f32[64,2048]{1,0:T(8,128)} %shard_map.100.att_ref, bf16[64,2048]{1,0:T(8,128)(2,1)} %bitcast.11, bf16[2048]{0:T(1024)(128)(2,1)} %gain_ref.1, bf16[16,2048]{1,0:T(8,128)(2,1)} %bitcast.12, s32[8,64]{1,0:T(8,128)} %bitcast.13, bf16[1,2048,1536]{2,1,0:T(8,128)(2,1)} %gu_hbm.1, ...), custom_call_target="tpu_custom_call" | custom-call | tf_op jit(solution)/shard_map/pallas_call | solution.py:782
  120.0 1.7 %copy.12 = bf16[1,64,2048]{2,1,0:T(8,128)(2,1)} copy(bf16[1,64,2048]{2,1,0:T(8,128)(2,1)} %bitcast.8) | data formatting | bytes 524288

commit v2 on v1

--- a/solution.py
+++ b/solution.py
@@ -15,16 +15,12 @@
 EPSILON = 1e-06
 MESH = pl.DeviceIdType.MESH
 CHUNKS = 4
-AG_KINDS = (0, 1, 0, 0)
-RS_KINDS = (0, 1, 0, 0)
-AG_FIRST = 1.0
-AG_CHUNK = 1.0
-AG_HOP = 1.0
-FFN_START = 4.0
-FFN_CHUNK = 1.0
-FFN_SPAN = 0.9
-RS_LAG = 0.5
-RS_HOP = 1.0
+AG_KINDS = (0, 1, 0, 1)
+ORDER = (
+    0, 1, 0, 1, 0, 2, 0, 0, 1, 2, 1, 0, 3, 0, 0, 0, 0, 0, 2, 1, 0, 1, 3, 2,
+    1, 0, 1, 1, 1, 1, 2, 1, 2, 3, 2, 2, 1, 2, 3, 2, 2, 0, 0, 3, 2, 3, 3, 3,
+    3, 2, 3, 3, 3, 1, 1, 0, 3, 2, 2, 1, 3, 3, 2, 3,
+)
 
 
 def bit_count(number):
@@ -383,16 +379,9 @@
     )(x, gates)
 
 
-def ag_time(k, stage):
-    return AG_CHUNK * k + AG_HOP * stage if stage else AG_FIRST * k
-
-
-def ffn_time(k, part):
-    return FFN_START + FFN_CHUNK * k + FFN_SPAN * part + 0.001
-
-
-def rs_time(k, stage):
-    return FFN_START + FFN_CHUNK * k + FFN_SPAN + RS_LAG + RS_HOP * stage
+def plain_order(counts, lag):
+    entries = [(step + lag * k, k) for k, count in enumerate(counts) for step in range(count)]
+    return [k for _, k in sorted(entries)]
 
 
 def moe_fits(devices, rows, width, hidden):
@@ -404,9 +393,9 @@
 
 
 def moe_kernel(
-    line, ag_kinds, rs_kinds,
+    line, ag_kinds,
     att_ref, res_ref, gain_ref, router_ref, ids_ref, gu_hbm, dn_hbm, o_ref,
-    gath, gu, dn, act, made, mrecv, part, yrecv, half, zrecv, held, ready,
+    gath, gu, dn, act, made, mrecv, part, yrecv, half, zrecv, held,
     w_sem, ag_send, ag_recv, m_send, m_recv, y_send, y_recv, z_send, z_recv,
 ):
     me = lax.axis_index("dev")
@@ -439,13 +428,20 @@
     for copy in copies:
         copy.start()
     barrier = pltpu.get_barrier_semaphore()
-    for way in range(4):
-        guarded(
-            allowed[way],
-            lambda way=way: pl.semaphore_signal(
-                barrier, inc=1, device_id={"dev": dest[way]}, device_id_type=MESH
-            ),
-        )
+    offsets = [sign * step for step in range(line - 1, 0, -1) for sign in (1, -1)]
+
+    def exists(offset):
+        if offset == 0:
+            return None
+        return z + offset >= 0 if offset < 0 else z + offset < line
+
+    def greet_one(other):
+        pl.semaphore_signal(barrier, inc=1, device_id={"dev": other}, device_id_type=MESH)
+
+    greet_one(dest[YMATE])
+    greet_one(dest[MATE])
+    for offset in offsets:
+        pl.when(exists(offset))(lambda offset=offset: greet_one(me + 4 * offset))
 
     stream = (res_ref[...].astype(jnp.float32) + att_ref[...]).astype(jnp.bfloat16)
     values = stream.astype(jnp.float32)
@@ -474,20 +470,13 @@
         gath[k, mine, 0:width] = normed[k * R : (k + 1) * R]
         gath[k, mine, width:padded] = extra[k * R : (k + 1) * R]
 
-    pl.semaphore_wait(
-        barrier, 2 + (z > 0).astype(jnp.int32) + (z + 1 < line).astype(jnp.int32)
-    )
+    pl.semaphore_wait(barrier, line + 1)
 
     span = 2 * line - 1
     started = []
 
     def label(side, offset):
         return side * span + offset + line - 1
-
-    def exists(offset):
-        if offset == 0:
-            return None
-        return z + offset >= 0 if offset < 0 else z + offset < line
 
     def slab(k, side, offset):
         column = y if side == 0 else 1 - y
@@ -625,25 +614,26 @@
         )
 
     def y_copy(k):
-        if rs_kinds[k] == 0:
-            source, target = part.at[k, 1 - y], yrecv.at[k]
-        else:
-            source, target = ready.at[k], yrecv.at[k, 0]
         return pltpu.make_async_remote_copy(
-            src_ref=source, dst_ref=target,
+            src_ref=part.at[k, 1 - y], dst_ref=yrecv.at[k],
             send_sem=y_send.at[k], recv_sem=y_recv.at[k],
             device_id={"dev": dest[YMATE]}, device_id_type=MESH,
         )
 
-    def z_copy(k, target, way):
-        if rs_kinds[k] == 0:
-            source, landing = half.at[k, target], zrecv.at[k, way, target, 0]
-        else:
-            source, landing = part.at[k, :, target], zrecv.at[k, way, target]
+    def z_copy(k, offset):
+        target = jnp.clip(z + offset, 0, line - 1)
         return pltpu.make_async_remote_copy(
-            src_ref=source, dst_ref=landing,
-            send_sem=z_send.at[k, way, target], recv_sem=z_recv.at[k, way, target],
-            device_id={"dev": dest[way]}, device_id_type=MESH,
+            src_ref=half.at[k, target], dst_ref=zrecv.at[k, line - 1 - offset],
+            send_sem=z_send.at[k, line - 1 + offset], recv_sem=z_recv.at[k, line - 1 - offset],
+            device_id={"dev": me + 4 * (target - z)}, device_id_type=MESH,
+        )
+
+    def z_arrived(k, offset):
+        where = zrecv.at[k, line - 1 + offset]
+        return pltpu.make_async_remote_copy(
+            src_ref=where, dst_ref=where,
+            send_sem=z_send.at[k, line - 1 + offset], recv_sem=z_recv.at[k, line - 1 + offset],
+            device_id={"dev": dest[MATE]}, device_id_type=MESH,
         )
 
     def merge(k):
@@ -656,9 +646,8 @@
                     made[k, ours, :].astype(jnp.float32)
                     + mrecv[k, at * R : (at + 1) * R, :].astype(jnp.float32)
                 ).astype(part.dtype)
-        if rs_kinds[k] == 0:
-            y_copy(k).start()
-            started.append((lambda: None, lambda: y_copy(k)))
+        y_copy(k).start()
+        started.append((lambda: None, lambda: y_copy(k)))
 
     def y_merge(k):
         y_copy(k).wait_recv()
@@ -667,100 +656,39 @@
                 part[k, y, place].astype(jnp.float32) + yrecv[k, place].astype(jnp.float32)
             ).astype(half.dtype)
 
-    def z_hop(k, hop):
-        for way in (RIGHT, LEFT):
-            here = hop if way == RIGHT else line - 1 - hop
-            if way == RIGHT:
-                targets = range(line - 1, here, -1)
-            else:
-                targets = range(0, here)
-
-            def body(way=way, here=here, targets=targets):
-                for target in targets:
-                    if hop:
-                        z_copy(k, target, way).wait_recv()
-                        if rs_kinds[k] == 0:
-                            half[k, target] = (
-                                half[k, target].astype(jnp.float32)
-                                + zrecv[k, way, target, 0].astype(jnp.float32)
-                            ).astype(half.dtype)
-                        else:
-                            for column in range(2):
-                                part[k, column, target] = (
-                                    part[k, column, target].astype(jnp.float32)
-                                    + zrecv[k, way, target, column].astype(jnp.float32)
-                                ).astype(part.dtype)
-                    z_copy(k, target, way).start()
-
-            for target in targets:
-                started.append(
-                    (
-                        lambda here=here: z == here,
-                        lambda target=target, way=way: z_copy(k, target, way),
-                    )
-                )
-            pl.when(z == here)(body)
-
-    def gather_z(k, column):
-        where = pl.ds(k * R, R)
-
-        def take(way):
-            side = 0 if rs_kinds[k] == 0 else column
-            held[where, :] = held[where, :] + zrecv[k, way, z, side].astype(jnp.float32)
-
-        pl.when(z > 0)(lambda: take(RIGHT))
-        pl.when(z + 1 < line)(lambda: take(LEFT))
-
-    def wait_z(k):
-        pl.when(z > 0)(lambda: z_copy(k, z, RIGHT).wait_recv())
-        pl.when(z + 1 < line)(lambda: z_copy(k, z, LEFT).wait_recv())
-
-    def cross(k):
-        wait_z(k)
-        other = part[k, 1 - y, z].astype(jnp.float32)
-        from_left = zrecv[k, RIGHT, z, 1 - y].astype(jnp.float32)
-        from_right = zrecv[k, LEFT, z, 1 - y].astype(jnp.float32)
-        other = other + jnp.where(z > 0, from_left, 0.0)
-        other = other + jnp.where(z + 1 < line, from_right, 0.0)
-        ready[k] = other.astype(ready.dtype)
-        y_copy(k).start()
-        started.append((lambda: None, lambda: y_copy(k)))
+    def z_scatter(k):
+        for offset in offsets:
+            pl.when(exists(offset))(lambda offset=offset: z_copy(k, offset).start())
+            started.append(
+                (lambda offset=offset: exists(offset), lambda offset=offset: z_copy(k, offset))
+            )
 
     def finish(k):
         where = pl.ds(k * R, R)
-        if rs_kinds[k] == 0:
-            wait_z(k)
-            held[where, :] = held[where, :] + half[k, z].astype(jnp.float32)
-            gather_z(k, 0)
-            o_ref[where, :] = held[where, :].astype(o_ref.dtype)
-        else:
-            held[where, :] = held[where, :] + part[k, y, z].astype(jnp.float32)
-            gather_z(k, y)
-            y_copy(k).wait_recv()
-            o_ref[where, :] = (
-                held[where, :] + yrecv[k, 0].astype(jnp.float32)
-            ).astype(o_ref.dtype)
-
-    def rs_stages(k):
-        hops = [functools.partial(z_hop, k, hop) for hop in range(line - 1)]
-        if rs_kinds[k] == 0:
-            middle = [lambda: y_merge(k)] + hops
-        else:
-            middle = hops + [lambda: cross(k)]
-        return [lambda: merge(k)] + middle + [lambda: finish(k)]
-
+        held[where, :] = held[where, :] + half[k, z].astype(jnp.float32)
+        for offset in reversed(offsets):
+
+            def add(offset=offset):
+                z_arrived(k, offset).wait_recv()
+                held[where, :] = held[where, :] + zrecv[k, line - 1 + offset].astype(jnp.float32)
+
+            pl.when(exists(offset))(add)
+        o_ref[where, :] = held[where, :].astype(o_ref.dtype)
+
+    rs_stages = [merge, y_merge, z_scatter, finish]
     pieces = [functools.partial(rise, start=start) for start in range(0, hidden, strip)]
     pieces += [functools.partial(fall, start=start) for start in range(0, width, wide)]
-    agenda = []
+    queues = []
     for k in range(chunks):
-        for stage in range(line + 1):
-            agenda.append((ag_time(k, stage), lambda k=k, stage=stage: ag_stage(k, stage)))
-        for number, piece in enumerate(pieces):
-            agenda.append((ffn_time(k, number / len(pieces)), lambda k=k, piece=piece: piece(k)))
-        for number, step in enumerate(rs_stages(k)):
-            agenda.append((rs_time(k, number), step))
-    for _, step in sorted(agenda, key=lambda entry: entry[0]):
-        step()
+        steps = [functools.partial(ag_stage, k, stage) for stage in range(line + 1)]
+        steps += [functools.partial(piece, k) for piece in pieces]
+        steps += [functools.partial(step, k) for step in rs_stages]
+        queues.append(steps)
+    order = ORDER
+    if [order.count(k) for k in range(chunks)] != [len(steps) for steps in queues]:
+        order = plain_order([len(steps) for steps in queues], line + 1 + len(pieces) // 2)
+    for k in order:
+        queues[k].pop(0)()
     for cond, copy in started:
         guarded(cond(), lambda copy=copy: copy().wait_send())
 
@@ -780,7 +708,7 @@
     dma = pltpu.SemaphoreType.DMA
     total = devices * R
     return pl.pallas_call(
-        functools.partial(moe_kernel, line, AG_KINDS, RS_KINDS),
+        functools.partial(moe_kernel, line, AG_KINDS),
         out_shape=jax.ShapeDtypeStruct((rows, width), kind),
         in_specs=[vmem] * 5 + [hbm] * 2,
         out_specs=vmem,
@@ -794,9 +722,8 @@
             pltpu.VMEM((CHUNKS, 2, line, R, width), kind),
             pltpu.VMEM((CHUNKS, line, R, width), kind),
             pltpu.VMEM((CHUNKS, line, R, width), kind),
-            pltpu.VMEM((CHUNKS, 2, line, 2, R, width), kind),
+            pltpu.VMEM((CHUNKS, span, R, width), kind),
             pltpu.VMEM((rows, width), jnp.float32),
-            pltpu.VMEM((CHUNKS, R, width), kind),
             dma((2,)),
             dma((CHUNKS, 2 * span, 4)),
             dma((CHUNKS, 4 * span)),
@@ -804,8 +731,8 @@
             dma((CHUNKS,)),
             dma((CHUNKS,)),
             dma((CHUNKS,)),
-            dma((CHUNKS, 2, line)),
-            dma((CHUNKS, 2, line)),
+            dma((CHUNKS, span)),
+            dma((CHUNKS, span)),
         ],
         compiler_params=pltpu.CompilerParams(collective_id=collective_id, has_side_effects=True),
     )(attended, residual, gain, router, ids, gate_up, down)

time: 122 us -> 108 us (0.89)
  Pallas kernels: 120 us -> 106 us
    pallas_call x1, Pallas kernels: 76.9 us -> 63.4 us  [moe(): pl.pallas_call(functools.partial(moe_kernel, line, AG_KINDS), out_shape=j...]
where the time goes in v2:
time: 108 us
  Pallas kernels  106 us (98%)
  local copies, waits for them, and re-layouts  1.67 us (2%)
    pallas_call x1, Pallas kernels, moe(): pl.pallas_call(functools.partial(moe_kernel, line, AG_KINDS), out_shape=j...  63.4 us
    pallas_call x1, Pallas kernels, attention(): pl.pallas_call(functools.partial(attention_kernel, unit, parts, bits), ou...  43.1 us

profile of v2, /device:TPU:0, one launch (start us, length us, event | category | flops | bytes accessed | tf_op | source)
XLA Modules:
  0.0 108.2 jit_solution(17461294585887112683)
XLA Ops:
  0.0 43.1 %shard_map.100.att_ref = f32[64,2048]{1,0:T(8,128)} custom-call(s32[2]{0:T(128)} %lengths_ref.1, bf16[512,512]{1,0:T(8,128)(2,1)} %bitcast.9, bf16[2,512,128]{2,1,0:T(8,128)(2,1)} %bitcast.10, bf16[256,2048]{1,0:T(8,128)(2,1)} %proj_ref.1), custom_call_target="tpu_custom_call" | custom-call | tf_op jit(solution)/shard_map/pallas_call | solution.py:255
  43.1 63.4 %shard_map.101 = bf16[64,2048]{1,0:T(8,128)(2,1)} custom-call(f32[64,2048]{1,0:T(8,128)} %shard_map.100.att_ref, bf16[64,2048]{1,0:T(8,128)(2,1)} %bitcast.11, bf16[2048]{0:T(1024)(128)(2,1)} %gain_ref.1, bf16[16,2048]{1,0:T(8,128)(2,1)} %bitcast.12, s32[8,64]{1,0:T(8,128)} %bitcast.13, bf16[1,2048,1536]{2,1,0:T(8,128)(2,1)} %gu_hbm.1, ...), custom_call_target="tpu_custom_call" | custom-call | tf_op jit(solution)/shard_map/pallas_call | solution.py:710
  106.5 1.7 %copy.12 = bf16[1,64,2048]{2,1,0:T(8,128)(2,1)} copy(bf16[1,64,2048]{2,1,0:T(8,128)(2,1)} %bitcast.8) | data formatting | bytes 524288

commit v3 on v2

--- a/solution.py
+++ b/solution.py
@@ -15,11 +15,13 @@
 EPSILON = 1e-06
 MESH = pl.DeviceIdType.MESH
 CHUNKS = 4
-AG_KINDS = (0, 1, 0, 1)
+ATTENTION_GROUPS = 8
+GATHER_SHARE = 6
+SCATTER_SHARE = 2
 ORDER = (
-    0, 1, 0, 1, 0, 2, 0, 0, 1, 2, 1, 0, 3, 0, 0, 0, 0, 0, 2, 1, 0, 1, 3, 2,
-    1, 0, 1, 1, 1, 1, 2, 1, 2, 3, 2, 2, 1, 2, 3, 2, 2, 0, 0, 3, 2, 3, 3, 3,
-    3, 2, 3, 3, 3, 1, 1, 0, 3, 2, 2, 1, 3, 3, 2, 3,
+    0, 1, 0, 1, 0, 3, 0, 1, 2, 0, 3, 0, 1, 0, 0, 0, 2, 0, 1, 0, 0, 3, 1, 1,
+    3, 2, 0, 1, 3, 1, 1, 1, 1, 2, 3, 3, 3, 3, 3, 3, 3, 1, 0, 2, 3, 2, 2, 2,
+    2, 2, 2, 2, 1, 2, 0, 3, 2, 3, 1, 2,
 )
 
 
@@ -120,7 +122,7 @@
         finish(o_ref)
 
 
-def attend_block(block, length, q_ref, halves, rows):
+def attend_block(block, length, q_ref, halves, rows, values_ready=None):
     heads = q_ref.shape[1] // HEAD_DIM
     picked = pl.ds(pl.multiple_of(block * rows, rows), rows)
     query = jnp.concatenate(
@@ -140,6 +142,8 @@
     old = jnp.exp(old - top)
     new = jnp.exp(new - top)
     total = jnp.sum(old, axis=1, keepdims=True) + jnp.sum(new, axis=1, keepdims=True)
+    if values_ready is not None:
+        values_ready()
     mixed = jnp.dot(old.astype(jnp.bfloat16), halves[0, 1], preferred_element_type=jnp.float32)
     mixed += jnp.dot(new.astype(jnp.bfloat16), halves[1, 1], preferred_element_type=jnp.float32)
     mixed = (mixed / total).astype(jnp.bfloat16)
@@ -171,15 +175,19 @@
     own_half.start()
     own_proj.start()
     pl.semaphore_wait(barrier, len(mates) + len(ranks))
-    kv_copy = pltpu.make_async_remote_copy(
-        src_ref=kv_ref,
-        dst_ref=halves.at[parity],
-        send_sem=kv_sem.at[0],
-        recv_sem=kv_sem.at[1],
-        device_id={"dev": ranks[0]},
-        device_id_type=MESH,
-    )
-    kv_copy.start()
+    kv_copies = [
+        pltpu.make_async_remote_copy(
+            src_ref=kv_ref.at[place],
+            dst_ref=halves.at[parity, place],
+            send_sem=kv_sem.at[place],
+            recv_sem=kv_sem.at[2 + place],
+            device_id={"dev": ranks[0]},
+            device_id_type=MESH,
+        )
+        for place in range(2)
+    ]
+    for copy in kv_copies:
+        copy.start()
     proj_copies = []
     for place, other in enumerate(mates):
         copy = pltpu.make_async_remote_copy(
@@ -193,7 +201,7 @@
         copy.start()
         proj_copies.append(copy)
     own_half.wait()
-    kv_copy.wait()
+    kv_copies[0].wait()
 
     blocks, rows, width = x.shape
     far = 1 << (len(bits) - 1)
@@ -207,14 +215,16 @@
         )
         for number, (order, cols) in enumerate(parts)
     ]
-    half = blocks // 2
+    groups = min(ATTENTION_GROUPS, blocks)
+    half = blocks // groups
     strip = math.gcd(width, 512)
-    for group in range(2):
+    for group in range(groups):
         for spot in range(half):
             mask = masks[group * half + spot]
             block = flipped(rank, subset(bits, mask))
             heads[spot * rows : (spot + 1) * rows, :] = attend_block(
-                block, length, q_ref, halves, rows
+                block, length, q_ref, halves, rows,
+                kv_copies[1].wait if group == 0 and spot == 0 else None,
             )
         if group == 0:
             own_proj.wait()
@@ -247,7 +257,7 @@
     bits = sorted(orders[0])
     blocks = 1 << len(bits)
     rows = tokens // blocks
-    cut = width * 3 // 4 // 128 * 128
+    cut = width * 13 // 16 // 128 * 128
     parts = [(orders[0], pl.ds(0, cut)), (orders[1], pl.ds(cut, width - cut))]
     mates = max((1 << unit) - 1, 1)
     kind = queries.dtype
@@ -260,13 +270,13 @@
         scratch_shapes=[
             pltpu.VMEM((2,) + key_values.shape, kind),
             pltpu.VMEM((out_proj.shape[0] << unit, width), kind),
-            pltpu.VMEM((tokens // 2, columns), kind),
+            pltpu.VMEM((tokens // min(ATTENTION_GROUPS, blocks), columns), kind),
             pltpu.VMEM((blocks, rows, width), kind),
             pltpu.VMEM((blocks - 1, rows, width), kind),
             pltpu.VMEM((max(blocks // 2 - 1, 1), rows, width), kind),
             pltpu.SemaphoreType.DMA((2, blocks - 1)),
             pltpu.SemaphoreType.DMA((2, blocks - 1)),
-            pltpu.SemaphoreType.DMA((2,)),
+            pltpu.SemaphoreType.DMA((4,)),
             pltpu.SemaphoreType.DMA((mates,)),
             pltpu.SemaphoreType.DMA((mates,)),
             pltpu.SemaphoreType.DMA((2,)),
@@ -393,10 +403,10 @@
 
 
 def moe_kernel(
-    line, ag_kinds,
+    line, gather_cut, scatter_cut,
     att_ref, res_ref, gain_ref, router_ref, ids_ref, gu_hbm, dn_hbm, o_ref,
-    gath, gu, dn, act, made, mrecv, part, yrecv, half, zrecv, held,
-    w_sem, ag_send, ag_recv, m_send, m_recv, y_send, y_recv, z_send, z_recv,
+    gath, gu, dn, act, made, mrecv, part, yrecv, half, zrecv, held, ready, ylate, zearly, cross,
+    w_sem, ag_send, ag_recv, pass_send, pass_recv, m_send, m_recv, y_send, y_recv, z_send, z_recv,
 ):
     me = lax.axis_index("dev")
     z, y, c = me // 4, (me // 2) % 2, me % 2
@@ -474,35 +484,42 @@
 
     span = 2 * line - 1
     started = []
+    gathered = [[] for _ in range(chunks)]
+    scattered = [[] for _ in range(chunks)]
+
+    def drain(pending):
+        while pending:
+            cond, copy = pending.pop(0)
+            guarded(cond(), lambda: copy().wait_send())
 
     def label(side, offset):
         return side * span + offset + line - 1
 
-    def slab(k, side, offset):
+    columns = [pl.ds(gather_cut, padded - gather_cut), pl.ds(0, gather_cut)]
+
+    def slab(k, lot, side, offset, core=None):
         column = y if side == 0 else 1 - y
-        return gath.at[k, pl.ds(spot(c, column, z + offset), R), :]
-
-    def ag_copy(k, side, offset, way):
+        core = c if core is None else core
+        return gath.at[k, pl.ds(spot(core, column, z + offset), R), columns[lot]]
+
+    def ag_copy(k, lot, side, offset, way):
         if way == RIGHT:
             landing = label(side, offset - 1)
         elif way == LEFT:
             landing = label(side, offset + 1)
-        elif way == YMATE:
+        else:
             landing = label(1 - side, offset)
-        else:
-            landing = 2 * span + label(side, offset)
-        where = slab(k, side, offset)
+        where = slab(k, lot, side, offset)
         return pltpu.make_async_remote_copy(
             src_ref=where, dst_ref=where,
-            send_sem=ag_send.at[k, label(side, offset), way],
-            recv_sem=ag_recv.at[k, landing],
+            send_sem=ag_send.at[k, lot, label(side, offset), way],
+            recv_sem=ag_recv.at[k, lot, landing],
             device_id={"dev": dest[way]}, device_id_type=MESH,
         )
 
-    def ag_ways(k, side, offset):
-        kind = ag_kinds[k]
+    def ag_ways(lot, side, offset):
         ways = []
-        if kind == 0:
+        if lot == 0:
             if side == 0:
                 if offset <= 0 and offset > 1 - line:
                     ways.append(RIGHT)
@@ -516,60 +533,60 @@
                 ways.append(RIGHT)
             if offset >= 0 and offset < line - 1:
                 ways.append(LEFT)
-        ways.append(MATE)
         return ways
 
-    def ag_step(k, side, offset):
+    def ag_step(k, lot, side, offset):
         def body():
             if side or offset:
-                arrived = slab(k, side, offset)
+                arrived = slab(k, lot, side, offset)
                 pltpu.make_async_remote_copy(
                     src_ref=arrived, dst_ref=arrived,
-                    send_sem=ag_send.at[k, label(side, offset), MATE],
-                    recv_sem=ag_recv.at[k, label(side, offset)],
+                    send_sem=ag_send.at[k, lot, label(side, offset), YMATE],
+                    recv_sem=ag_recv.at[k, lot, label(side, offset)],
                     device_id={"dev": dest[MATE]}, device_id_type=MESH,
                 ).wait_recv()
-            for way in ag_ways(k, side, offset):
-                copy = ag_copy(k, side, offset, way)
-                guarded(allowed[way], copy.start)
+            for way in ag_ways(lot, side, offset):
+                guarded(allowed[way], ag_copy(k, lot, side, offset, way).start)
 
         guarded(exists(offset), body)
-        for way in ag_ways(k, side, offset):
-            started.append(
+        for way in ag_ways(lot, side, offset):
+            gathered[k].append(
                 (
                     lambda way=way: both(exists(offset), allowed[way]),
-                    lambda way=way: ag_copy(k, side, offset, way),
+                    lambda way=way: ag_copy(k, lot, side, offset, way),
                 )
             )
 
     def ag_stage(k, stage):
-        if stage == 0:
-            ag_step(k, 0, 0)
-            return
-        if stage < line:
-            ag_step(k, 0, -stage)
-            ag_step(k, 0, stage)
-        if stage == 1:
-            ag_step(k, 1, 0)
-        else:
-            ag_step(k, 1, 1 - stage)
-            ag_step(k, 1, stage - 1)
+        for lot in range(2):
+            if stage == 0:
+                ag_step(k, lot, 0, 0)
+                continue
+            if stage < line:
+                ag_step(k, lot, 0, -stage)
+                ag_step(k, lot, 0, stage)
+            if stage == 1:
+                ag_step(k, lot, 1, 0)
+            else:
+                ag_step(k, lot, 1, 1 - stage)
+                ag_step(k, lot, 1, stage - 1)
+        if stage >= line - 1:
+            ag_pass(k, stage - line + 1).start()
+            gathered[k].append((lambda: None, lambda: ag_pass(k, stage - line + 1)))
+
+    def ag_pass(k, side, core=None):
+        column = y if side == 0 else 1 - y
+        core = c if core is None else core
+        where = gath.at[k, pl.ds(spot(core, column, 0), line * R), :]
+        return pltpu.make_async_remote_copy(
+            src_ref=where, dst_ref=where,
+            send_sem=pass_send.at[k, side], recv_sem=pass_recv.at[k, side],
+            device_id={"dev": dest[MATE]}, device_id_type=MESH,
+        )
 
     def mate_wait(k):
         for side in range(2):
-            for offset in range(1 - line, line):
-                column = y if side == 0 else 1 - y
-
-                def body(side=side, offset=offset, column=column):
-                    where = gath.at[k, pl.ds(spot(1 - c, column, z + offset), R), :]
-                    pltpu.make_async_remote_copy(
-                        src_ref=where, dst_ref=where,
-                        send_sem=ag_send.at[k, label(side, offset), MATE],
-                        recv_sem=ag_recv.at[k, 2 * span + label(side, offset)],
-                        device_id={"dev": dest[MATE]}, device_id_type=MESH,
-                    ).wait_recv()
-
-                guarded(exists(offset), body)
+            ag_pass(k, side, 1 - c).wait_recv()
 
     core_rows = total // 2
     strip = math.gcd(hidden, 256)
@@ -589,7 +606,7 @@
                 x, gu[:, hidden + start : hidden + start + strip],
                 preferred_element_type=jnp.float32,
             )
-            act[:, start : start + strip] = (gate / (1.0 + jnp.exp(-gate)) * up).astype(act.dtype)
+            act[k, :, start : start + strip] = (gate / (1.0 + jnp.exp(-gate)) * up).astype(act.dtype)
 
     def fall(k, start):
         tail = gath[k, :, width:padded].astype(jnp.float32)
@@ -598,12 +615,12 @@
         weight = jnp.sum(jnp.where(chosen, tail, 0.0), axis=1, keepdims=True)
         if True:
             produced = jnp.dot(
-                act[...], dn[:, start : start + wide], preferred_element_type=jnp.float32
+                act[k], dn[:, start : start + wide], preferred_element_type=jnp.float32
             )
             made[k, :, start : start + wide] = (weight * produced).astype(made.dtype)
         if start + wide == width:
             mate_copy(k).start()
-            started.append((lambda: None, lambda: mate_copy(k)))
+            scattered[k].append((lambda: None, lambda: mate_copy(k)))
 
     def mate_copy(k):
         theirs = pl.ds(pl.multiple_of((1 - c) * core_rows, core_rows), core_rows)
@@ -613,30 +630,57 @@
             device_id={"dev": dest[MATE]}, device_id_type=MESH,
         )
 
-    def y_copy(k):
+    late = pl.ds(0, scatter_cut)
+    soon = pl.ds(scatter_cut, width - scatter_cut)
+
+    def y_copy(k, lot):
+        if lot == 0:
+            source, target = part.at[k, 1 - y, :, :, soon], yrecv.at[k]
+        else:
+            source, target = ready.at[k], ylate.at[k]
         return pltpu.make_async_remote_copy(
-            src_ref=part.at[k, 1 - y], dst_ref=yrecv.at[k],
-            send_sem=y_send.at[k], recv_sem=y_recv.at[k],
+            src_ref=source, dst_ref=target,
+            send_sem=y_send.at[k, lot], recv_sem=y_recv.at[k, lot],
             device_id={"dev": dest[YMATE]}, device_id_type=MESH,
         )
 
-    def z_copy(k, offset):
+    def y_start(k, lot):
+        y_copy(k, lot).start()
+        pending = scattered[k] if lot == 0 else started
+        pending.append((lambda: None, lambda: y_copy(k, lot)))
+
+    def z_copy(k, lot, offset):
         target = jnp.clip(z + offset, 0, line - 1)
+        slot = line - 1 - offset
+        if lot == 0:
+            source, landing = half.at[k, target], zrecv.at[k, slot]
+        else:
+            source, landing = part.at[k, :, target, :, late], zearly.at[k, slot]
         return pltpu.make_async_remote_copy(
-            src_ref=half.at[k, target], dst_ref=zrecv.at[k, line - 1 - offset],
-            send_sem=z_send.at[k, line - 1 + offset], recv_sem=z_recv.at[k, line - 1 - offset],
+            src_ref=source, dst_ref=landing,
+            send_sem=z_send.at[k, lot, line - 1 + offset], recv_sem=z_recv.at[k, lot, slot],
             device_id={"dev": me + 4 * (target - z)}, device_id_type=MESH,
         )
 
-    def z_arrived(k, offset):
-        where = zrecv.at[k, line - 1 + offset]
-        return pltpu.make_async_remote_copy(
+    def z_arrive(k, lot, offset):
+        slot = line - 1 + offset
+        where = (zrecv if lot == 0 else zearly).at[k, slot]
+        pltpu.make_async_remote_copy(
             src_ref=where, dst_ref=where,
-            send_sem=z_send.at[k, line - 1 + offset], recv_sem=z_recv.at[k, line - 1 + offset],
+            send_sem=z_send.at[k, lot, slot], recv_sem=z_recv.at[k, lot, slot],
             device_id={"dev": dest[MATE]}, device_id_type=MESH,
-        )
+        ).wait_recv()
+
+    def z_start(k, lot):
+        for offset in offsets:
+            pl.when(exists(offset))(lambda offset=offset: z_copy(k, lot, offset).start())
+            pending = scattered[k] if lot == 1 else started
+            pending.append(
+                (lambda offset=offset: exists(offset), lambda offset=offset: z_copy(k, lot, offset))
+            )
 
     def merge(k):
+        drain(gathered[k])
         mate_copy(k).wait_recv()
         for column in range(2):
             for place in range(line):
@@ -646,36 +690,50 @@
                     made[k, ours, :].astype(jnp.float32)
                     + mrecv[k, at * R : (at + 1) * R, :].astype(jnp.float32)
                 ).astype(part.dtype)
-        y_copy(k).start()
-        started.append((lambda: None, lambda: y_copy(k)))
-
-    def y_merge(k):
-        y_copy(k).wait_recv()
+        y_start(k, 0)
+        z_start(k, 1)
+
+    def middle(k):
+        y_copy(k, 0).wait_recv()
         for place in range(line):
             half[k, place] = (
-                part[k, y, place].astype(jnp.float32) + yrecv[k, place].astype(jnp.float32)
+                part[k, y, place, :, soon].astype(jnp.float32)
+                + yrecv[k, place].astype(jnp.float32)
             ).astype(half.dtype)
-
-    def z_scatter(k):
-        for offset in offsets:
-            pl.when(exists(offset))(lambda offset=offset: z_copy(k, offset).start())
-            started.append(
-                (lambda offset=offset: exists(offset), lambda offset=offset: z_copy(k, offset))
-            )
+        z_start(k, 0)
+        where = pl.ds(k * R, R)
+        cross[...] = part[k, 1 - y, z, :, late].astype(jnp.float32)
+        held[where, late] = held[where, late] + part[k, y, z, :, late].astype(jnp.float32)
+        for offset in reversed(offsets):
+
+            def add(offset=offset):
+                z_arrive(k, 1, offset)
+                slot = line - 1 + offset
+                cross[...] = cross[...] + zearly[k, slot, 1 - y].astype(jnp.float32)
+                held[where, late] = held[where, late] + zearly[k, slot, y].astype(jnp.float32)
+
+            pl.when(exists(offset))(add)
+        ready[k] = cross[...].astype(ready.dtype)
+        y_start(k, 1)
 
     def finish(k):
+        drain(scattered[k])
         where = pl.ds(k * R, R)
-        held[where, :] = held[where, :] + half[k, z].astype(jnp.float32)
+        held[where, soon] = held[where, soon] + half[k, z].astype(jnp.float32)
         for offset in reversed(offsets):
 
             def add(offset=offset):
-                z_arrived(k, offset).wait_recv()
-                held[where, :] = held[where, :] + zrecv[k, line - 1 + offset].astype(jnp.float32)
+                z_arrive(k, 0, offset)
+                held[where, soon] = held[where, soon] + zrecv[k, line - 1 + offset].astype(
+                    jnp.float32
+                )
 
             pl.when(exists(offset))(add)
+        y_copy(k, 1).wait_recv()
+        held[where, late] = held[where, late] + ylate[k].astype(jnp.float32)
         o_ref[where, :] = held[where, :].astype(o_ref.dtype)
 
-    rs_stages = [merge, y_merge, z_scatter, finish]
+    rs_stages = [merge, middle, finish]
     pieces = [functools.partial(rise, start=start) for start in range(0, hidden, strip)]
     pieces += [functools.partial(fall, start=start) for start in range(0, width, wide)]
     queues = []
@@ -689,8 +747,7 @@
         order = plain_order([len(steps) for steps in queues], line + 1 + len(pieces) // 2)
     for k in order:
         queues[k].pop(0)()
-    for cond, copy in started:
-        guarded(cond(), lambda copy=copy: copy().wait_send())
+    drain(started)
 
 
 def moe(attended, residual, gain, router, ids, gate_up, down, collective_id):
@@ -707,8 +764,11 @@
     hbm = pl.BlockSpec(memory_space=pl.ANY)
     dma = pltpu.SemaphoreType.DMA
     total = devices * R
+    gather_cut = width * GATHER_SHARE // 16 // 128 * 128
+    scatter_cut = width * SCATTER_SHARE // 16 // 128 * 128
+    soon = width - scatter_cut
     return pl.pallas_call(
-        functools.partial(moe_kernel, line, AG_KINDS),
+        functools.partial(moe_kernel, line, gather_cut, scatter_cut),
         out_shape=jax.ShapeDtypeStruct((rows, width), kind),
         in_specs=[vmem] * 5 + [hbm] * 2,
         out_specs=vmem,
@@ -716,23 +776,29 @@
             pltpu.VMEM((CHUNKS, total, padded), kind),
             pltpu.VMEM(gate_up.shape[1:], kind),
             pltpu.VMEM(down.shape[1:], kind),
-            pltpu.VMEM((total, hidden), kind),
+            pltpu.VMEM((CHUNKS, total, hidden), kind),
             pltpu.VMEM((CHUNKS, total, width), kind),
             pltpu.VMEM((CHUNKS, total // 2, width), kind),
             pltpu.VMEM((CHUNKS, 2, line, R, width), kind),
-            pltpu.VMEM((CHUNKS, line, R, width), kind),
-            pltpu.VMEM((CHUNKS, line, R, width), kind),
-            pltpu.VMEM((CHUNKS, span, R, width), kind),
+            pltpu.VMEM((CHUNKS, line, R, soon), kind),
+            pltpu.VMEM((CHUNKS, line, R, soon), kind),
+            pltpu.VMEM((CHUNKS, span, R, soon), kind),
             pltpu.VMEM((rows, width), jnp.float32),
+            pltpu.VMEM((CHUNKS, R, scatter_cut), kind),
+            pltpu.VMEM((CHUNKS, R, scatter_cut), kind),
+            pltpu.VMEM((CHUNKS, span, 2, R, scatter_cut), kind),
+            pltpu.VMEM((R, scatter_cut), jnp.float32),
             dma((2,)),
-            dma((CHUNKS, 2 * span, 4)),
-            dma((CHUNKS, 4 * span)),
+            dma((CHUNKS, 2, 2 * span, 3)),
+            dma((CHUNKS, 2, 2 * span)),
+            dma((CHUNKS, 2)),
+            dma((CHUNKS, 2)),
             dma((CHUNKS,)),
             dma((CHUNKS,)),
-            dma((CHUNKS,)),
-            dma((CHUNKS,)),
-            dma((CHUNKS, span)),
-            dma((CHUNKS, span)),
+            dma((CHUNKS, 2)),
+            dma((CHUNKS, 2)),
+            dma((CHUNKS, 2, span)),
+            dma((CHUNKS, 2, span)),
         ],
         compiler_params=pltpu.CompilerParams(collective_id=collective_id, has_side_effects=True),
     )(attended, residual, gain, router, ids, gate_up, down)

time: 108 us -> 106 us (0.981)
  Pallas kernels: 106 us -> 104 us
    pallas_call x1, Pallas kernels: 63.4 us -> 61.6 us  [moe(): pl.pallas_call(functools.partial(moe_kernel, line, gather_cut, scatter_cu...]
where the time goes in v3:
time: 106 us; the launch traced here: 105 us
  Pallas kernels  104 us (98%)
  local copies, waits for them, and re-layouts  1.67 us (2%)
    pallas_call x1, Pallas kernels, moe(): pl.pallas_call(functools.partial(moe_kernel, line, gather_cut, scatter_cu...  61.6 us
    pallas_call x1, Pallas kernels, attention(): pl.pallas_call(functools.partial(attention_kernel, unit, parts, bits), ou...  42.1 us

profile of v3, /device:TPU:0, one launch (start us, length us, event | category | flops | bytes accessed | tf_op | source)
XLA Modules:
  0.0 105.4 jit_solution(3531926755332392906)
XLA Ops:
  0.0 42.1 %shard_map.100.att_ref = f32[64,2048]{1,0:T(8,128)} custom-call(s32[2]{0:T(128)} %lengths_ref.1, bf16[512,512]{1,0:T(8,128)(2,1)} %bitcast.9, bf16[2,512,128]{2,1,0:T(8,128)(2,1)} %bitcast.10, bf16[256,2048]{1,0:T(8,128)(2,1)} %proj_ref.1), custom_call_target="tpu_custom_call" | custom-call | tf_op jit(solution)/shard_map/pallas_call | solution.py:265
  42.1 61.6 %shard_map.101 = bf16[64,2048]{1,0:T(8,128)(2,1)} custom-call(f32[64,2048]{1,0:T(8,128)} %shard_map.100.att_ref, bf16[64,2048]{1,0:T(8,128)(2,1)} %bitcast.11, bf16[2048]{0:T(1024)(128)(2,1)} %gain_ref.1, bf16[16,2048]{1,0:T(8,128)(2,1)} %bitcast.12, s32[8,64]{1,0:T(8,128)} %bitcast.13, bf16[1,2048,1536]{2,1,0:T(8,128)(2,1)} %gu_hbm.1, ...), custom_call_target="tpu_custom_call" | custom-call | tf_op jit(solution)/shard_map/pallas_call | solution.py:770
  103.7 1.7 %copy.12 = bf16[1,64,2048]{2,1,0:T(8,128)(2,1)} copy(bf16[1,64,2048]{2,1,0:T(8,128)(2,1)} %bitcast.8) | data formatting | bytes 524288

commit v4 on v3

--- a/solution.py
+++ b/solution.py
@@ -16,12 +16,12 @@
 MESH = pl.DeviceIdType.MESH
 CHUNKS = 4
 ATTENTION_GROUPS = 8
-GATHER_SHARE = 6
-SCATTER_SHARE = 2
+GATHER_SHARE = 7
+SCATTER_SHARE = 3
 ORDER = (
-    0, 1, 0, 1, 0, 3, 0, 1, 2, 0, 3, 0, 1, 0, 0, 0, 2, 0, 1, 0, 0, 3, 1, 1,
-    3, 2, 0, 1, 3, 1, 1, 1, 1, 2, 3, 3, 3, 3, 3, 3, 3, 1, 0, 2, 3, 2, 2, 2,
-    2, 2, 2, 2, 1, 2, 0, 3, 2, 3, 1, 2,
+    0, 1, 0, 2, 0, 1, 0, 2, 0, 3, 0, 1, 0, 0, 0, 0, 2, 0, 0, 1, 3, 2, 0, 1,
+    3, 2, 1, 1, 1, 1, 1, 1, 1, 2, 2, 2, 2, 0, 2, 3, 2, 2, 1, 3, 2, 3, 3, 3,
+    3, 3, 3, 3, 1, 0, 3, 2, 3, 1, 2, 3,
 )
 
 
@@ -682,15 +682,16 @@
     def merge(k):
         drain(gathered[k])
         mate_copy(k).wait_recv()
-        for column in range(2):
+        for column in (1 - y, y):
             for place in range(line):
                 at = column * line + place
                 ours = pl.ds(pl.multiple_of(c * core_rows + at * R, R), R)
+                theirs = pl.ds(pl.multiple_of(at * R, R), R)
                 part[k, column, place] = (
-                    made[k, ours, :].astype(jnp.float32)
-                    + mrecv[k, at * R : (at + 1) * R, :].astype(jnp.float32)
+                    made[k, ours, :].astype(jnp.float32) + mrecv[k, theirs, :].astype(jnp.float32)
                 ).astype(part.dtype)
-        y_start(k, 0)
+            if column is not y:
+                y_start(k, 0)
         z_start(k, 1)
 
     def middle(k):

time: 106 us -> 106 us (level)
  no operation moved by 1% of the time
where the time goes in v4:
time: 106 us; the launch traced here: 105 us
  Pallas kernels  104 us (98%)
  local copies, waits for them, and re-layouts  1.67 us (2%)
    pallas_call x1, Pallas kernels, moe(): pl.pallas_call(functools.partial(moe_kernel, line, gather_cut, scatter_cu...  61.6 us
    pallas_call x1, Pallas kernels, attention(): pl.pallas_call(functools.partial(attention_kernel, unit, parts, bits), ou...  42.1 us

profile of v4, /device:TPU:0, one launch (start us, length us, event | category | flops | bytes accessed | tf_op | source)
XLA Modules:
  0.0 105.3 jit_solution(13364369854628321940)
XLA Ops:
  0.0 42.1 %shard_map.100.att_ref = f32[64,2048]{1,0:T(8,128)} custom-call(s32[2]{0:T(128)} %lengths_ref.1, bf16[512,512]{1,0:T(8,128)(2,1)} %bitcast.9, bf16[2,512,128]{2,1,0:T(8,128)(2,1)} %bitcast.10, bf16[256,2048]{1,0:T(8,128)(2,1)} %proj_ref.1), custom_call_target="tpu_custom_call" | custom-call | tf_op jit(solution)/shard_map/pallas_call | solution.py:265
  42.1 61.6 %shard_map.101 = bf16[64,2048]{1,0:T(8,128)(2,1)} custom-call(f32[64,2048]{1,0:T(8,128)} %shard_map.100.att_ref, bf16[64,2048]{1,0:T(8,128)(2,1)} %bitcast.11, bf16[2048]{0:T(1024)(128)(2,1)} %gain_ref.1, bf16[16,2048]{1,0:T(8,128)(2,1)} %bitcast.12, s32[8,64]{1,0:T(8,128)} %bitcast.13, bf16[1,2048,1536]{2,1,0:T(8,128)(2,1)} %gu_hbm.1, ...), custom_call_target="tpu_custom_call" | custom-call | tf_op jit(solution)/shard_map/pallas_call | solution.py:771
  103.7 1.7 %copy.12 = bf16[1,64,2048]{2,1,0:T(8,128)(2,1)} copy(bf16[1,64,2048]{2,1,0:T(8,128)(2,1)} %bitcast.8) | data formatting | bytes 524288
